TPU v7x, 8 devices: a whole 2x2x1 slice. The times are simulated.
8 devices in a mesh: dp: 1 (over z), tp: 8 (over y, x, core).
Axes of the slice: x: 2, y: 2, z: 1, core: 2. Of those that a mesh axis runs over, the one named last changes fastest.
Arguments:
- x: bfloat16 [32, 256, 1536], P('dp', 'tp')
- d_out: bfloat16 [32, 256, 1536], P('dp', 'tp')
- ln1_gain: float32 [1536], replicated
- ln1_bias: float32 [1536], replicated
- w_q: bfloat16 [1536, 16, 96], P(None, 'tp')
- b_q: bfloat16 [16, 96], P('tp')
- w_k: bfloat16 [1536, 16, 96], P(None, 'tp')
- w_v: bfloat16 [1536, 16, 96], P(None, 'tp')
- b_v: bfloat16 [16, 96], P('tp')
- w_o: bfloat16 [16, 96, 1536], P('tp')
- b_o: bfloat16 [1536], replicated
- ln2_gain: float32 [1536], replicated
- ln2_bias: float32 [1536], replicated
- w_1: bfloat16 [1536, 6144], P(None, 'tp')
- b_1: bfloat16 [6144], P('tp')
- w_2: bfloat16 [6144, 1536], P('tp')
- b_2: bfloat16 [1536], replicated
Outputs:
- output 1: bfloat16 [32, 256, 1536], P('dp', 'tp')
- output 2: bfloat16 [32, 256, 1536], P('dp', 'tp')
- output 3: float32 [1536], P('dp')
- output 4: float32 [1536], P('dp')
- output 5: bfloat16 [1536, 16, 96], P('dp', 'tp')
- output 6: bfloat16 [16, 96], P(('dp', 'tp'))
- output 7: bfloat16 [1536, 16, 96], P('dp', 'tp')
- output 8: bfloat16 [1536, 16, 96], P('dp', 'tp')
- output 9: bfloat16 [16, 96], P(('dp', 'tp'))
- output 10: bfloat16 [16, 96, 1536], P(('dp', 'tp'))
- output 11: bfloat16 [1536], P('dp')
- output 12: float32 [1536], P('dp')
- output 13: float32 [1536], P('dp')
- output 14: bfloat16 [1536, 6144], P('dp', 'tp')
- output 15: bfloat16 [6144], P(('dp', 'tp'))
- output 16: bfloat16 [6144, 1536], P(('dp', 'tp'))
- output 17: bfloat16 [1536], P('dp')
All inputs are finite; a program needn't handle non-finite values.
Results may differ from a plain program's by a relative error of at most 0.0195979.
Values are sent between devices in bfloat16 or wider.
A program may use at most 1 GiB of HBM per device.

v0:
```python
import math
import jax
import jax.numpy as jnp
from jax import lax
from jax.sharding import PartitionSpec as P

LN_EPS = 1e-6


def layer_norm(rows, ln_gain, ln_bias):
    row_mean = jnp.mean(rows, axis=-1, keepdims=True)
    centered = rows - row_mean
    variance = jnp.mean(centered * centered, axis=-1, keepdims=True)
    return centered * lax.rsqrt(variance + LN_EPS) * ln_gain + ln_bias


def gelu_tanh(pre_act):
    return jax.nn.gelu(pre_act, approximate=True)


def attention_core(queries, keys, values):
    att_scale = 1.0 / math.sqrt(queries.shape[-1])
    scores = jnp.einsum('bqhd,bkhd->bhqk', queries, keys, preferred_element_type=jnp.float32) * att_scale
    probs = jax.nn.softmax(scores, axis=-1).astype(jnp.bfloat16)
    mixed = jnp.einsum('bhqk,bkhd->bqhd', probs, values, preferred_element_type=jnp.float32)
    return mixed.astype(jnp.bfloat16)


def token_sum(grad_rows):
    return jnp.sum(grad_rows, axis=(0, 1), dtype=jnp.float32)


def solution(mesh):
    act_spec = P('dp', 'tp', None)
    replicated = P()
    head_w = P(None, 'tp', None)
    head_b = P('tp', None)
    grad_head_w = P('dp', 'tp', None)
    grad_head_b = P(('dp', 'tp'), None)
    grad_vec = P('dp')
    in_specs = (act_spec, act_spec, replicated, replicated, head_w, head_b, head_w, head_w, head_b,
                P('tp', None, None), replicated, replicated, replicated, P(None, 'tp'), P('tp'), P('tp', None), replicated)
    out_specs = (act_spec, act_spec, grad_vec, grad_vec, grad_head_w, grad_head_b, grad_head_w, grad_head_w, grad_head_b,
                 P(('dp', 'tp'), None, None), grad_vec, grad_vec, grad_vec, P('dp', 'tp'), P(('dp', 'tp')),
                 P(('dp', 'tp'), None), grad_vec)

    def gather_tokens(local_rows):
        return lax.all_gather(local_rows, 'tp', axis=1, tiled=True)

    def scatter_sum(part_sum):
        return lax.psum_scatter(part_sum, 'tp', scatter_dimension=1, tiled=True)

    def layer_step(x, d_out, ln1_gain, ln1_bias, w_q, b_q, w_k, w_v, b_v, w_o, b_o, ln2_gain, ln2_bias, w_1, b_1, w_2, b_2):
        x_f32 = x.astype(jnp.float32)
        h_one_f, ln1_pull = jax.vjp(layer_norm, x_f32, ln1_gain, ln1_bias)
        h_one = gather_tokens(h_one_f.astype(jnp.bfloat16))
        queries = (jnp.einsum('bnw,whd->bnhd', h_one, w_q, preferred_element_type=jnp.float32) + b_q).astype(jnp.bfloat16)
        keys = jnp.einsum('bnw,whd->bnhd', h_one, w_k, preferred_element_type=jnp.float32).astype(jnp.bfloat16)
        values = (jnp.einsum('bnw,whd->bnhd', h_one, w_v, preferred_element_type=jnp.float32) + b_v).astype(jnp.bfloat16)
        mixed, attn_pull = jax.vjp(attention_core, queries, keys, values)
        attn_out = scatter_sum(jnp.einsum('bnhd,hdw->bnw', mixed, w_o, preferred_element_type=jnp.float32))
        x_mid = (x_f32 + attn_out + b_o).astype(jnp.bfloat16)
        mid_f32 = x_mid.astype(jnp.float32)
        h_two_f, ln2_pull = jax.vjp(layer_norm, mid_f32, ln2_gain, ln2_bias)
        h_two = gather_tokens(h_two_f.astype(jnp.bfloat16))
        pre_act = (jnp.einsum('bnw,wf->bnf', h_two, w_1, preferred_element_type=jnp.float32) + b_1).astype(jnp.bfloat16)
        hidden_f, gelu_pull = jax.vjp(gelu_tanh, pre_act.astype(jnp.float32))
        hidden = hidden_f.astype(jnp.bfloat16)
        mlp_out = scatter_sum(jnp.einsum('bnf,fw->bnw', hidden, w_2, preferred_element_type=jnp.float32))
        y_out = (mid_f32 + mlp_out + b_2).astype(jnp.bfloat16)

        d_out_all = gather_tokens(d_out)
        d_hidden = jnp.einsum('bnw,fw->bnf', d_out_all, w_2, preferred_element_type=jnp.float32).astype(jnp.bfloat16)
        grad_w_2 = jnp.einsum('bnf,bnw->fw', hidden, d_out_all, preferred_element_type=jnp.float32).astype(jnp.bfloat16)
        (d_pre_f,) = gelu_pull(d_hidden.astype(jnp.float32))
        d_pre = d_pre_f.astype(jnp.bfloat16)
        grad_b_1 = token_sum(d_pre).astype(jnp.bfloat16)
        grad_w_1 = jnp.einsum('bnw,bnf->wf', h_two, d_pre, preferred_element_type=jnp.float32).astype(jnp.bfloat16)
        d_h_two = scatter_sum(jnp.einsum('bnf,wf->bnw', d_pre, w_1, preferred_element_type=jnp.float32)).astype(jnp.bfloat16)
        d_mid_ln, g_ln2_gain, g_ln2_bias = ln2_pull(d_h_two.astype(jnp.float32))
        d_mid = (d_out.astype(jnp.float32) + d_mid_ln).astype(jnp.bfloat16)
        d_mid_all = gather_tokens(d_mid)
        d_mixed = jnp.einsum('bnw,hdw->bnhd', d_mid_all, w_o, preferred_element_type=jnp.float32).astype(jnp.bfloat16)
        grad_w_o = jnp.einsum('bnhd,bnw->hdw', mixed, d_mid_all, preferred_element_type=jnp.float32).astype(jnp.bfloat16)
        d_query, d_key, d_value = attn_pull(d_mixed)
        grad_b_q = token_sum(d_query).astype(jnp.bfloat16)
        grad_b_v = token_sum(d_value).astype(jnp.bfloat16)
        grad_w_q = jnp.einsum('bnw,bnhd->whd', h_one, d_query, preferred_element_type=jnp.float32).astype(jnp.bfloat16)
        grad_w_k = jnp.einsum('bnw,bnhd->whd', h_one, d_key, preferred_element_type=jnp.float32).astype(jnp.bfloat16)
        grad_w_v = jnp.einsum('bnw,bnhd->whd', h_one, d_value, preferred_element_type=jnp.float32).astype(jnp.bfloat16)
        d_h_one_part = (jnp.einsum('bnhd,whd->bnw', d_query, w_q, preferred_element_type=jnp.float32)
                        + jnp.einsum('bnhd,whd->bnw', d_key, w_k, preferred_element_type=jnp.float32)
                        + jnp.einsum('bnhd,whd->bnw', d_value, w_v, preferred_element_type=jnp.float32))
        d_h_one = scatter_sum(d_h_one_part).astype(jnp.bfloat16)
        d_in_ln, g_ln1_gain, g_ln1_bias = ln1_pull(d_h_one.astype(jnp.float32))
        grad_x = (d_mid.astype(jnp.float32) + d_in_ln).astype(jnp.bfloat16)
        vec_sums = lax.psum(jnp.stack([g_ln1_gain, g_ln1_bias, token_sum(d_mid), g_ln2_gain, g_ln2_bias, token_sum(d_out)]), 'tp')
        return (y_out, grad_x, vec_sums[0], vec_sums[1], grad_w_q, grad_b_q, grad_w_k, grad_w_v, grad_b_v, grad_w_o,
                vec_sums[2].astype(jnp.bfloat16), vec_sums[3], vec_sums[4], grad_w_1, grad_b_1, grad_w_2,
                vec_sums[5].astype(jnp.bfloat16))

    return jax.shard_map(layer_step, mesh=mesh, in_specs=in_specs, out_specs=out_specs, check_vma=False)
```

profile of v0, /device:TPU:0, one launch (start us, length us, event | category | flops | bytes accessed | tf_op | source)
XLA Modules:
  0.0 1983.6 jit_solution(10338738554035651037)
XLA Ops:
  7.3 2.5 convert_reduce_fusion.3
  9.9 2.9 fusion.55
  14.0 2.5 fusion.52
  17.0 122.2 %all-gather.5.cloned.1.call-done = bf16[32,256,1536]{2,1,0:T(8,128)(2,1)} async-done(((bf16[32,32,1536]{2,1,0:T(8,128)(2,1)}), bf16[32,256,1536]{2,1,0:T(8,128)(2,1)}) %all-gather.5.cloned.1.call-update) | async-done | bytes 25165840 | tf_op jit(solution)/shard_map/all_gather | solution.py:48
  139.2 14.2 fusion.129
  153.3 14.1 add_convert_fusion.1
  167.5 10.9 fusion.158
  178.4 6.8 divide_convert_fusion
  185.3 16.1 add_convert_fusion.2
  201.3 1.6 copy-done.9
  202.9 3.1 convolution_convert_fusion.3
  206.0 22.0 %convolution_bitcast_fusion = f32[32,256,1536]{2,1,0:T(8,128)} fusion(bf16[32,2,96,256]{3,2,1,0:T(8,128)(2,1)} %convolution_convert_fusion.3, bf16[2,96,1536]{2,1,0:T(8,128)(2,1)S(1)} %copy-done.18), kind=kOutput, calls=%fused_computation.10 | convolution fusion | flops 4831838208 | bytes 54067200 | tf_op jit(solution)/shard_map/bnhd,hdw->bnw/dot_general | solution.py:61
  228.7 274.0 %reduce-scatter.5.cloned.1.call-done = f32[32,32,1536]{2,1,0:T(8,128)} async-done(((f32[32,256,1536]{2,1,0:T(8,128)}), f32[32,32,1536]{2,1,0:T(8,128)}) %reduce-scatter.5.cloned.1.call-update) | async-done | bytes 6291472 | tf_op jit(solution)/shard_map/reduce_scatter | solution.py:51
  502.7 4.7 convert_reduce_fusion.2
  507.4 1.0 fusion.59
  509.7 2.5 fusion.50
  512.9 119.2 %all-gather.7.cloned.1.call-done = bf16[32,256,1536]{2,1,0:T(8,128)(2,1)} async-done(((bf16[32,32,1536]{2,1,0:T(8,128)(2,1)}), bf16[32,256,1536]{2,1,0:T(8,128)(2,1)}) %all-gather.7.cloned.1.call-update) | async-done | bytes 25165840 | tf_op jit(solution)/shard_map/all_gather | solution.py:48
  632.0 26.9 %add_convert_fusion = bf16[32,256,768]{2,1,0:T(8,128)(2,1)} fusion(f32[768]{0:T(1024)S(1)} %convert_element_type.173, bf16[32,256,1536]{2,1,0:T(8,128)(2,1)} %all-gather.7.cloned.1.call-done, bf16[1536,768]{1,0:T(8,128)(2,1)} %param.30), kind=kOutput, calls=%fused_computation.37 | convolution fusion | flops 19339935744 | bytes 40111104 | tf_op jit(solution)/shard_map/bnw,wf->bnf/dot_general | solution.py:66
  659.0 94.4 %all-gather.9.cloned.1.call-done = bf16[32,256,1536]{2,1,0:T(8,128)(2,1)} async-done(((bf16[32,32,1536]{2,1,0:T(8,128)(2,1)}), bf16[32,256,1536]{2,1,0:T(8,128)(2,1)}) %all-gather.9.cloned.1.call-update) | async-done | bytes 25165840 | tf_op jit(solution)/shard_map/all_gather | solution.py:48
  753.4 41.4 %fusion.159 = (bf16[768]{0:T(1024)(128)(2,1)}, bf16[32,256,768]{2,1,0:T(8,128)(2,1)}) fusion(bf16[32,256,768]{2,1,0:T(8,128)(2,1)} %add_convert_fusion, bf16[32,256,1536]{2,1,0:T(8,128)(2,1)} %all-gather.9.cloned.1.call-done, bf16[768,1536]{1,0:T(8,128)(2,1)S(1)} %copy-done), kind=kOutput, calls=%fused_computation.166 | convolution fusion | flops 19478347776 | bytes 52692480 | tf_op jit(solution)/shard_map/bnw,fw->bnf/dot_general | solution.py:73
  794.8 31.2 %fusion.123 = f32[32,256,1536]{2,1,0:T(8,128)} fusion(bf16[32,256,768]{2,1,0:T(8,128)(2,1)} %get-tuple-element.48, bf16[1536,768]{1,0:T(8,128)(2,1)} %param.30), kind=kOutput, calls=%fused_computation.129 | convolution fusion | flops 19327352832 | bytes 65273856 | tf_op jit(solution)/shard_map/bnf,wf->bnw/dot_general | solution.py:79
  826.1 31.7 %fusion.121 = f32[32,256,1536]{2,1,0:T(8,128)} fusion(bf16[768,1536]{1,0:T(8,128)(2,1)S(1)} %copy-done, bf16[32,256,768]{2,1,0:T(8,128)(2,1)} %add_convert_fusion), kind=kOutput, calls=%fused_computation.127 | convolution fusion | flops 19390267392 | bytes 65273856 | tf_op jit(solution)/shard_map/bnf,fw->bnw/dot_general | solution.py:69
  858.5 242.2 %reduce-scatter.9.cloned.1.call-done = f32[32,32,1536]{2,1,0:T(8,128)} async-done(((f32[32,256,1536]{2,1,0:T(8,128)}), f32[32,32,1536]{2,1,0:T(8,128)}) %reduce-scatter.9.cloned.1.call-update) | async-done | bytes 6291472 | tf_op jit(solution)/shard_map/reduce_scatter | solution.py:51
  1100.7 5.9 convert_reduce_fusion.1
  1106.7 4.0 fusion.63
  1110.8 267.9 %reduce-scatter.7.cloned.1.call-done = f32[32,32,1536]{2,1,0:T(8,128)} async-done(((f32[32,256,1536]{2,1,0:T(8,128)}), f32[32,32,1536]{2,1,0:T(8,128)}) %reduce-scatter.7.cloned.1.call-update) | async-done | bytes 6291472 | tf_op jit(solution)/shard_map/reduce_scatter | solution.py:51
  1378.7 10.1 convert_reduce_fusion.4
  1389.0 119.7 %all-gather.11.cloned.1.call-done = bf16[32,256,1536]{2,1,0:T(8,128)(2,1)} async-done(((bf16[32,32,1536]{2,1,0:T(8,128)(2,1)}), bf16[32,256,1536]{2,1,0:T(8,128)(2,1)}) %all-gather.11.cloned.1.call-update) | async-done | bytes 25165840 | tf_op jit(solution)/shard_map/all_gather | solution.py:48
  1508.7 13.2 fusion.132
  1521.8 1.7 copy-done.11
  1523.6 8.2 bitcast_reduce_fusion
  1531.8 11.8 fusion.32
  1543.6 13.1 convolution_convert_fusion.1
  1556.8 12.5 bitcast_reduce_fusion.1
  1569.2 21.5 %fusion.70 = f32[32,256,1536,1]{2,1,3,0:T(8,128)} fusion(bf16[32,2,256,96]{2,3,1,0:T(8,128)(2,1)} %convolution_convert_fusion.1, bf16[1536,2,96]{0,2,1:T(8,128)(2,1)S(1)} %copy-done.21), kind=kOutput, calls=%fused_computation.107 | convolution fusion | flops 4831838208 | bytes 54067200 | tf_op jit(solution)/shard_map/bnhd,whd->bnw/dot_general | solution.py:92
  1590.8 21.5 %fusion.73 = f32[32,256,1536,1]{2,1,3,0:T(8,128)} fusion(bf16[32,2,256,96]{2,3,1,0:T(8,128)(2,1)} %get-tuple-element.44, bf16[1536,2,96]{0,2,1:T(8,128)(2,1)S(1)} %copy-done.23), kind=kOutput, calls=%fused_computation.111 | convolution fusion | flops 4831838208 | bytes 54067200 | tf_op jit(solution)/shard_map/bnhd,whd->bnw/dot_general | solution.py:91
  1612.3 50.8 %bitcast_add_fusion = f32[32,256,1536]{2,1,0:T(8,128)} fusion(f32[32,256,1536,1]{2,1,3,0:T(8,128)} %fusion.70, f32[32,256,1536,1]{2,1,3,0:T(8,128)} %fusion.73, bf16[32,2,96,256]{3,2,1,0:T(8,128)(2,1)} %get-tuple-element.46, bf16[1536,2,96]{0,2,1:T(8,128)(2,1)S(1)} %copy-done.15), kind=kOutput, calls=%fused_computation.1 | convolution fusion | flops 4857004032 | bytes 154730496 | tf_op jit(solution)/shard_map/bnhd,whd->bnw/dot_general | solution.py:93
  1663.1 26.0 %bitcast_convert_fusion.1 = bf16[1536,768]{1,0:T(8,128)(2,1)} fusion(bf16[32,256,1536]{2,1,0:T(8,128)(2,1)} %all-gather.7.cloned.1.call-done, bf16[32,256,768]{2,1,0:T(8,128)(2,1)} %get-tuple-element.48), kind=kOutput, calls=%fused_computation.100 | convolution fusion | flops 19328532480 | bytes 40108032 | tf_op jit(solution)/shard_map/bnw,bnf->wf/dot_general | solution.py:78
  1689.1 36.4 %bitcast_convert_fusion = bf16[768,1536]{1,0:T(8,128)(2,1)} fusion(bf16[32,256,1536]{2,1,0:T(8,128)(2,1)} %all-gather.9.cloned.1.call-done, bf16[32,256,768]{2,1,0:T(8,128)(2,1)} %add_convert_fusion), kind=kOutput, calls=%fused_computation.99 | convolution fusion | flops 19391447040 | bytes 40108032 | tf_op jit(solution)/shard_map/bnf,bnw->fw/dot_general | solution.py:74
  1725.5 12.5 fusion.100
  1738.1 11.8 fusion.105
  1749.9 11.8 fusion.115
  1761.7 11.7 fusion.110
  1773.4 164.4 %reduce-scatter.11.cloned.1.call-done = f32[32,32,1536]{2,1,0:T(8,128)} async-done(((f32[32,256,1536]{2,1,0:T(8,128)}), f32[32,32,1536]{2,1,0:T(8,128)}) %reduce-scatter.11.cloned.1.call-update) | async-done | bytes 6291472 | tf_op jit(solution)/shard_map/reduce_scatter | solution.py:51
  1937.8 4.7 convert_reduce_fusion
  1942.5 3.6 fusion.64
  1946.2 22.6 %psum.7 = f32[6,1536]{1,0:T(8,128)S(1)} all-reduce(f32[6,1536]{1,0:T(8,128)S(1)} %stack.27), channel_id=1, replica_groups=mesh['dp'=1,'tp'=8] {'tp'}, use_global_device_ids=true, to_apply=%region_21.0 | all-reduce | flops 9216 | bytes 73728 | tf_op jit(solution)/shard_map/psum | solution.py:97
  1969.6 6.4 fusion.54
  (143 shorter events, 6.7 us)
Async XLA Ops:
  7.2 746.2 %copy-start = (bf16[768,1536]{1,0:T(8,128)(2,1)S(1)}, bf16[768,1536]{1,0:T(8,128)(2,1)}, u32[]{:S(2)}) copy-start(bf16[768,1536]{1,0:T(8,128)(2,1)} %param.32) | copy-start | bytes 7077892
  7.2 6.8 copy-start.38
  7.2 6.8 copy-start.44
  7.2 131.9 %all-gather.5.cloned.1.call-start = ((), (), s32[]{:S(2)}) async-start(), calls=%async_computation.4 | async-start | bytes 28311552 | tf_op jit(solution)/shard_map/all_gather | solution.py:48
  7.3 6.8 copy-start.2
  9.8 3.6 copy-start.16
  9.8 7.1 copy-start.49
  9.8 7.1 copy-start.50
  9.9 129.3 %copy-start.20 = (bf16[1536,2,96]{0,2,1:T(8,128)(2,1)S(1)}, bf16[1536,2,96]{0,2,1:T(8,128)(2,1)}, u32[]{:S(2)}) copy-start(bf16[1536,2,96]{0,2,1:T(8,128)(2,1)} %param.23) | copy-start | bytes 1769476
  16.5 486.2 %reduce-scatter.5.cloned.1.call-start = ((), (), s32[]{:S(2)}) async-start(), calls=%async_computation.5 | async-start | bytes 56623104 | tf_op jit(solution)/shard_map/reduce_scatter | solution.py:51
  17.0 136.4 %copy-start.22 = (bf16[1536,2,96]{0,2,1:T(8,128)(2,1)S(1)}, bf16[1536,2,96]{0,2,1:T(8,128)(2,1)}, u32[]{:S(2)}) copy-start(bf16[1536,2,96]{0,2,1:T(8,128)(2,1)} %param.21) | copy-start | bytes 1769476
  178.4 6.9 copy-start.28
  178.4 6.8 copy-start.14
  185.2 16.1 copy-start.4
  228.0 404.0 %all-gather.7.cloned.1.call-start = ((), (), s32[]{:S(2)}) async-start(), calls=%async_computation.6 | async-start | bytes 28311552 | tf_op jit(solution)/shard_map/all_gather | solution.py:48
  228.7 281.0 %copy-start.36 = (f32[1536]{0:T(1024)S(1)}, f32[1536]{0:T(1024)}, u32[]{:S(2)}) copy-start(f32[1536]{0:T(1024)} %param.28) | copy-start | bytes 18436
  228.7 281.0 %copy-start.45 = (f32[1536]{0:T(1024)S(1)}, f32[1536]{0:T(1024)}, u32[]{:S(2)}) copy-start(f32[1536]{0:T(1024)} %param.29) | copy-start | bytes 18436
  512.2 241.2 %all-gather.9.cloned.1.call-start = ((), (), s32[]{:S(2)}) async-start(), calls=%async_computation.8 | async-start | bytes 28311552 | tf_op jit(solution)/shard_map/all_gather | solution.py:48
  512.8 587.9 %reduce-scatter.9.cloned.1.call-start = ((), (), s32[]{:S(2)}) async-start(), calls=%async_computation.9 | async-start | bytes 56623104 | tf_op jit(solution)/shard_map/reduce_scatter | solution.py:51
  826.1 552.6 %reduce-scatter.7.cloned.1.call-start = ((), (), s32[]{:S(2)}) async-start(), calls=%async_computation.7 | async-start | bytes 56623104 | tf_op jit(solution)/shard_map/reduce_scatter | solution.py:51
  857.9 242.9 %copy-start.25 = (f32[32,32]{1,0:T(8,128)S(1)}, f32[32,32]{1,0:T(8,128)}, u32[]{:S(2)}) copy-start(f32[32,32]{1,0:T(8,128)} %copy-done.24) | copy-start | bytes 12292
  857.9 242.9 %copy-start.37 = (f32[1536]{0:T(1024)S(1)}, f32[1536]{0:T(1024)}, u32[]{:S(2)}) copy-start(f32[1536]{0:T(1024)} %param.28) | copy-start | bytes 18436
  857.9 650.8 %all-gather.11.cloned.1.call-start = ((), (), s32[]{:S(2)}) async-start(), calls=%async_computation.10 | async-start | bytes 28311552 | tf_op jit(solution)/shard_map/all_gather | solution.py:48
  858.5 248.1 %copy-start.35 = (f32[32,32]{1,0:T(8,128)S(1)}, f32[32,32]{1,0:T(8,128)}, u32[]{:S(2)}) copy-start(f32[32,32]{1,0:T(8,128)} %copy-done.34) | copy-start | bytes 12292
  858.5 248.1 %copy-start.31 = (f32[32,32]{1,0:T(8,128)S(1)}, f32[32,32]{1,0:T(8,128)}, u32[]{:S(2)}) copy-start(f32[32,32]{1,0:T(8,128)} %copy-done.30) | copy-start | bytes 12292
  1100.7 6.0 copy-start.6
  1106.7 4.1 copy-start.8
  1110.7 278.1 %copy-start.29 = (f32[32,2,256]{2,1,0:T(2,128)S(1)}, f32[32,2,256]{2,1,0:T(2,128)}, u32[]{:S(2)}) copy-start(f32[32,2,256]{2,1,0:T(2,128)} %copy-done.28) | copy-start | bytes 196612
  1110.8 397.9 %copy-start.19 = (bf16[2,96,1536]{2,1,0:T(8,128)(2,1)S(1)}, bf16[2,96,1536]{2,1,0:T(8,128)(2,1)}, u32[]{:S(2)}) copy-start(bf16[2,96,1536]{2,1,0:T(8,128)(2,1)} %param.26) | copy-start | bytes 1769476
  1388.8 548.9 %reduce-scatter.11.cloned.1.call-start = ((), (), s32[]{:S(2)}) async-start(), calls=%async_computation.11 | async-start | bytes 56623104 | tf_op jit(solution)/shard_map/reduce_scatter | solution.py:51
  1543.6 13.1 copy-start.51
  1556.8 12.5 copy-start.21
  1569.2 21.5 %copy-start.23 = (bf16[1536,2,96]{0,2,1:T(8,128)(2,1)S(1)}, bf16[1536,2,96]{0,2,1:T(8,128)(2,1)}, u32[]{:S(2)}) copy-start(bf16[1536,2,96]{0,2,1:T(8,128)(2,1)} %param.21) | copy-start | bytes 1769476
  1590.8 21.5 %copy-start.15 = (bf16[1536,2,96]{0,2,1:T(8,128)(2,1)S(1)}, bf16[1536,2,96]{0,2,1:T(8,128)(2,1)}, u32[]{:S(2)}) copy-start(bf16[1536,2,96]{0,2,1:T(8,128)(2,1)} %param.24) | copy-start | bytes 1769476
  1689.1 36.4 %copy-start.40 = (f32[1536]{0:T(1024)S(1)}, f32[1536]{0:T(1024)}, u32[]{:S(2)}) copy-start(f32[1536]{0:T(1024)} %get-tuple-element.21) | copy-start | bytes 18436
  1689.1 36.4 %copy-start.41 = (f32[1536]{0:T(1024)S(1)}, f32[1536]{0:T(1024)}, u32[]{:S(2)}) copy-start(f32[1536]{0:T(1024)} %get-tuple-element.17) | copy-start | bytes 18436
  1689.1 36.4 %copy-start.43 = (f32[1536]{0:T(1024)S(1)}, f32[1536]{0:T(1024)}, u32[]{:S(2)}) copy-start(f32[1536]{0:T(1024)} %get-tuple-element.31) | copy-start | bytes 18436
  1689.1 36.5 %copy-start.42 = (f32[1536]{0:T(1024)S(1)}, f32[1536]{0:T(1024)}, u32[]{:S(2)}) copy-start(f32[1536]{0:T(1024)} %get-tuple-element.37) | copy-start | bytes 18436
  1725.5 12.5 copy-start.10
  1738.1 11.8 copy-start.13
  1749.9 11.8 copy-start.12
  1761.7 176.1 %copy-start.17 = (f32[32,32]{1,0:T(8,128)S(1)}, f32[32,32]{1,0:T(8,128)}, u32[]{:S(2)}) copy-start(f32[32,32]{1,0:T(8,128)} %copy-done.16) | copy-start | bytes 12292
  1761.7 176.1 %copy-start.39 = (f32[1536]{0:T(1024)S(1)}, f32[1536]{0:T(1024)}, u32[]{:S(2)}) copy-start(f32[1536]{0:T(1024)} %param.19) | copy-start | bytes 18436
  1773.4 169.1 %copy-start.33 = (f32[32,32]{1,0:T(8,128)S(1)}, f32[32,32]{1,0:T(8,128)}, u32[]{:S(2)}) copy-start(f32[32,32]{1,0:T(8,128)} %copy-done.32) | copy-start | bytes 12292
  1773.4 169.1 %copy-start.27 = (f32[32,32]{1,0:T(8,128)S(1)}, f32[32,32]{1,0:T(8,128)}, u32[]{:S(2)}) copy-start(f32[32,32]{1,0:T(8,128)} %copy-done.26) | copy-start | bytes 12292
  1937.8 4.8 copy-start.3
  1942.5 3.7 copy-start.7
  1969.6 7.0 copy-start.1
  (12 other events, 16.8 us)
Sparse Core Ops, SparseCore 0:
  16.7 122.4 all-gather.4
  228.2 274.4 reduce-scatter.4
  512.4 119.6 all-gather.6
  633.7 119.6 all-gather.8
  826.2 274.4 reduce-scatter.8
  1104.1 274.5 reduce-scatter.6
  1389.0 119.6 all-gather.10
  1663.2 274.4 reduce-scatter.10
where the time goes:
time: 1990 us; the launch traced here: 1980 us
  waiting for transfers between devices  1400 us (70%)
  matrix products  474 us (24%)
  other arithmetic  57.9 us (3%)
  blocking collectives  22.6 us (1%)
    reduce_scatter x4, waiting for transfers between devices, scatter_sum(): return lax.psum_scatter(part_sum, 'tp', scatter_dimension=1, tiled=True)  948 us
    all_gather x4, waiting for transfers between devices, gather_tokens(): return lax.all_gather(local_rows, 'tp', axis=1, tiled=True)  455 us
    dot_general x1, matrix products, layer_step(): jnp.einsum('bnhd,whd->bnw', d_value, w_v, preferred_element_type=jnp.floa...  50.8 us
    dot_general x1, matrix products, layer_step(): jnp.einsum('bnw,fw->bnf', d_out_all, w_2, preferred_element_type=jnp.floa...  41.4 us
  transfers between devices with their start and end apart: 8, of which 8 were waited for; matrix products, arithmetic and copies ran while one was open for 9% of the time, Pallas kernels for 0%

commit v1 on v0

v1 whole, which is shorter than its diff:
```python
import functools
import math
import jax
import jax.numpy as jnp
from jax import lax
from jax.experimental import pallas as pl
from jax.experimental.pallas import tpu as pltpu
from jax.sharding import Mesh, PartitionSpec as P

LN_EPS = 1e-6
BF = jnp.bfloat16
F32 = jnp.float32


def layer_norm(rows, ln_gain, ln_bias):
    row_mean = jnp.mean(rows, axis=-1, keepdims=True)
    centered = rows - row_mean
    variance = jnp.mean(centered * centered, axis=-1, keepdims=True)
    return centered * lax.rsqrt(variance + LN_EPS) * ln_gain + ln_bias


def gelu_tanh(pre_act):
    return jax.nn.gelu(pre_act, approximate=True)


HEADS_PER_STEP = 4


def head_cols(head, which, heads, hd):
    dev, h = divmod(head, heads)
    start = (dev * 3 + which) * heads * hd + h * hd
    return slice(start, start + hd)


def probs_of(q, k, scale):
    s = lax.dot_general(q, k, (((1,), (1,)), ((), ())), preferred_element_type=F32) * scale
    e = jnp.exp(s - jnp.max(s, axis=-1, keepdims=True))
    return e / jnp.sum(e, axis=-1, keepdims=True)


def attn_fwd_kernel(heads, hd, qkv_ref, out_ref):
    scale = 1.0 / math.sqrt(hd)
    outs = []
    qkv = qkv_ref[...]
    for head in range(HEADS_PER_STEP):
        q, k, v = (qkv[:, head_cols(head, i, heads, hd)] for i in range(3))
        p = probs_of(q, k, scale).astype(BF)
        outs.append(dot_nn(p, v).astype(BF))
    out_ref[...] = jnp.concatenate(outs, axis=1)


def attn_bwd_kernel(heads, hd, qkv_ref, da_ref, out_ref):
    scale = 1.0 / math.sqrt(hd)
    pieces = {}
    qkv, d_mixed = qkv_ref[...], da_ref[...]
    for head in range(HEADS_PER_STEP):
        q, k, v = (qkv[:, head_cols(head, i, heads, hd)] for i in range(3))
        da = d_mixed[:, head * hd:(head + 1) * hd]
        p = probs_of(q, k, scale)
        dv = dot_tn(p.astype(BF), da)
        dp = dot_nt(da, v).astype(BF).astype(F32)
        ds = p * (dp - jnp.sum(dp * p, axis=-1, keepdims=True))
        ds = (ds * scale).astype(BF)
        grads = (dot_nn(ds, k), dot_tn(ds, q), dv)
        for i in range(3):
            pieces[head_cols(head, i, heads, hd).start] = grads[i].astype(BF)
    out_ref[...] = jnp.concatenate([pieces[c] for c in sorted(pieces)], axis=1)


def attention_call(body, images, tokens, out_cols, args, hd, flops):
    steps = args[0].shape[1] // (3 * hd * HEADS_PER_STEP)

    def spec(cols):
        return pl.BlockSpec((tokens, cols // steps), lambda b, g: (b, g))

    return pl.pallas_call(
        body, grid=(images, steps),
        in_specs=[spec(a.shape[1]) for a in args], out_specs=spec(out_cols),
        out_shape=jax.ShapeDtypeStruct((images * tokens, out_cols), BF),
        compiler_params=pltpu.CompilerParams(dimension_semantics=('parallel', 'parallel')),
        cost_estimate=pl.CostEstimate(flops=flops, transcendentals=0,
                                      bytes_accessed=2 * images * tokens * (out_cols + sum(a.shape[1] for a in args))),
    )(*args)


def dot_nt(a, b):
    return lax.dot_general(a, b, (((1,), (1,)), ((), ())), preferred_element_type=F32)


def dot_nn(a, b):
    return lax.dot_general(a, b, (((1,), (0,)), ((), ())), preferred_element_type=F32)


def dot_tn(a, b):
    return lax.dot_general(a, b, (((0,), (0,)), ((), ())), preferred_element_type=F32)


def row_sum(rows):
    return jnp.sum(rows, axis=0, dtype=F32)


def solution(mesh):
    chips = mesh.shape['tp'] // 2
    mesh = Mesh(mesh.devices.reshape(mesh.shape['dp'], chips, 2), ('dp', 'chip', 'core'))
    TP = ('chip', 'core')
    act_spec = P('dp', TP, None)
    replicated = P()
    head_w = P(None, TP, None)
    head_b = P(TP, None)
    grad_head_w = P('dp', TP, None)
    grad_head_b = P(('dp',) + TP, None)
    grad_vec = P('dp')
    in_specs = (act_spec, act_spec, replicated, replicated, head_w, head_b, head_w, head_w, head_b,
                P(TP, None, None), replicated, replicated, replicated, P(None, TP), P(TP), P(TP, None), replicated)
    out_specs = (act_spec, act_spec, grad_vec, grad_vec, grad_head_w, grad_head_b, grad_head_w, grad_head_w, grad_head_b,
                 P(('dp',) + TP, None, None), grad_vec, grad_vec, grad_vec, P('dp', TP), P(('dp',) + TP),
                 P(('dp',) + TP, None), grad_vec)
    tp = chips * 2

    def gather(rows, axes=('core', 'chip')):
        return lax.all_gather(rows, axes, axis=0, tiled=True)

    def weight_grad(cotangent, acts):
        core = lax.axis_index('core')
        half = cotangent.shape[1] // 2

        def part(which):
            return dot_tn(lax.dynamic_slice_in_dim(cotangent, which * half, half, axis=1), acts)

        other = lax.ppermute(part(1 - core), 'core', [(0, 1), (1, 0)])
        own = part(core) + other
        return lax.psum_scatter(own, 'chip', scatter_dimension=0, tiled=True).astype(BF)

    def to_images(rows):
        return lax.all_to_all(rows, TP, 0, 1, tiled=True)

    def to_tokens(rows):
        me = lax.axis_index(TP)
        img, toks, width = rows.shape
        toks //= tp

        def piece(dev):
            return lax.dynamic_slice_in_dim(rows, dev * toks, toks, axis=1)

        out = jnp.zeros((img * tp, toks, width), rows.dtype)
        out = lax.dynamic_update_slice_in_dim(out, piece(me), me * img, axis=0)
        for k in range(1, tp):
            got = lax.ppermute(piece(me ^ k), TP, [(i, i ^ k) for i in range(tp)])
            out = lax.dynamic_update_slice_in_dim(out, got, (me ^ k) * img, axis=0)
        return out

    def layer_step(x, d_out, ln1_gain, ln1_bias, w_q, b_q, w_k, w_v, b_v, w_o, b_o, ln2_gain, ln2_bias, w_1, b_1, w_2, b_2):
        images, toks, width = x.shape
        heads, hd = w_q.shape[1], w_q.shape[2]
        img = images // tp
        rows = img * toks * tp
        lw = heads * hd
        me = lax.axis_index(TP)
        me_cc = lax.axis_index(('core', 'chip'))

        def head_rows(w):
            return w.transpose(1, 2, 0).reshape(lw, width)

        w_qkv = gather(jnp.concatenate([head_rows(w_q), head_rows(w_k), head_rows(w_v)], axis=0))

        def bias_rows(bias):
            return bias.astype(F32).reshape(-1, hd)

        b_own = jnp.concatenate([bias_rows(b_q), jnp.zeros((heads, hd), F32), bias_rows(b_v), bias_rows(b_1)], axis=0)
        b_rows = lax.all_gather(b_own, ('core', 'chip'), axis=0, tiled=False)
        b_qkv = b_rows[:, :3 * heads].reshape(3 * lw * tp)
        b_1all = b_rows[:, 3 * heads:].reshape(b_1.shape[0] * tp)
        w_oall = gather(w_o.reshape(lw, width))
        w_1all = gather(w_1.T)
        w_2all = gather(w_2)
        d_out_all = gather(d_out, TP)

        x_img = to_images(x).reshape(rows, width)
        x_f32 = x_img.astype(F32)
        h_one_f, ln1_pull = jax.vjp(layer_norm, x_f32, ln1_gain, ln1_bias)
        h_one = h_one_f.astype(BF)
        qkv = (dot_nt(h_one, w_qkv) + b_qkv.astype(F32)).astype(BF)
        attn_flops = 4 * rows * toks * tp * tp * lw
        mixed_rows = attention_call(functools.partial(attn_fwd_kernel, heads, hd), img, toks * tp,
                                    tp * lw, (qkv,), hd, attn_flops)
        x_mid = (x_f32 + dot_nn(mixed_rows, w_oall) + b_o.astype(F32)).astype(BF)
        mid_f32 = x_mid.astype(F32)
        h_two_f, ln2_pull = jax.vjp(layer_norm, mid_f32, ln2_gain, ln2_bias)
        h_two = h_two_f.astype(BF)
        h_two_all = gather(h_two, TP)

        pre_act = (dot_nt(h_two, w_1all) + b_1all.astype(F32)).astype(BF)
        hidden_f, gelu_pull = jax.vjp(gelu_tanh, pre_act.astype(F32))
        hidden = hidden_f.astype(BF)
        y_img = (mid_f32 + dot_nn(hidden, w_2all) + b_2.astype(F32)).astype(BF)
        y_out = to_tokens(y_img.reshape(img, toks * tp, width))
        d_stack = d_out_all.reshape(tp, images, toks, width)
        d_img = lax.dynamic_slice_in_dim(d_stack, me * img, img, axis=1).transpose(1, 0, 2, 3).reshape(rows, width)
        d_hidden = lax.optimization_barrier(dot_nt(d_img, w_2all).astype(BF))
        (d_pre_f,) = gelu_pull(d_hidden.astype(F32))
        d_pre = d_pre_f.astype(BF)
        d_h_two = dot_nn(d_pre, w_1all).astype(BF)
        d_mid_ln, g_ln2_gain, g_ln2_bias = ln2_pull(d_h_two.astype(F32))
        d_mid = (d_img.astype(F32) + d_mid_ln).astype(BF)
        d_mixed = dot_nt(d_mid, w_oall).astype(BF)
        grad_w_o = weight_grad(mixed_rows, d_mid).reshape(w_o.shape)
        d_qkv = attention_call(functools.partial(attn_bwd_kernel, heads, hd), img, toks * tp,
                               3 * tp * lw, (qkv, d_mixed), hd, 5 * attn_flops // 2)
        part_b_qkv = row_sum(d_qkv)
        grad_w_qkv = weight_grad(d_qkv, h_one).reshape(3, heads, hd, width)
        grad_w_q, grad_w_k, grad_w_v = (grad_w_qkv[i].transpose(2, 0, 1) for i in range(3))
        d_h_one = dot_nn(d_qkv, w_qkv).astype(BF)
        d_in_ln, g_ln1_gain, g_ln1_bias = ln1_pull(d_h_one.astype(F32))
        grad_x_img = (d_mid.astype(F32) + d_in_ln).astype(BF)
        grad_x = to_tokens(grad_x_img.reshape(img, toks * tp, width))

        t_pre = (dot_nn(h_two_all, w_1) + b_1.astype(F32)).astype(BF)
        t_hidden_f, t_pull = jax.vjp(gelu_tanh, t_pre.astype(F32))
        t_hidden = t_hidden_f.astype(BF)
        d_ord = d_stack.transpose(1, 0, 2, 3).reshape(images * tp * toks, width)
        t_d_hidden = lax.optimization_barrier(dot_nt(d_ord, w_2).astype(BF))
        (t_d_pre_f,) = t_pull(t_d_hidden.astype(F32))
        t_d_pre = t_d_pre_f.astype(BF)
        grad_b_1 = row_sum(t_d_pre).astype(BF)
        grad_w_1 = dot_tn(h_two_all, t_d_pre).astype(BF)
        grad_w_2 = dot_tn(t_hidden, d_ord).astype(BF)
        vec_parts = jnp.concatenate([g_ln1_gain, g_ln1_bias, row_sum(d_mid), g_ln2_gain, g_ln2_bias, row_sum(d_img), part_b_qkv])
        vec_parts, grad_w_1, grad_w_2 = lax.optimization_barrier((vec_parts, grad_w_1, grad_w_2))
        vec_sums = lax.psum(vec_parts.reshape(9, width), TP).reshape(9 * width)
        grad_b_qkv = lax.dynamic_slice_in_dim(vec_sums[6 * width:], me_cc * 3 * lw, 3 * lw).astype(BF).reshape(3, heads, hd)
        vec_sums = vec_sums[:6 * width].reshape(6, width)
        return (y_out, grad_x, vec_sums[0], vec_sums[1], grad_w_q, grad_b_qkv[0], grad_w_k, grad_w_v, grad_b_qkv[2], grad_w_o,
                vec_sums[2].astype(BF), vec_sums[3], vec_sums[4], grad_w_1, grad_b_1, grad_w_2,
                vec_sums[5].astype(BF))

    return jax.shard_map(layer_step, mesh=mesh, in_specs=in_specs, out_specs=out_specs, check_vma=False)
```

time: 1990 us -> 1020 us (0.51)
  waiting for transfers between devices: 1400 us -> 359 us
  matrix products: 474 us -> 362 us
  Pallas kernels: 0 us -> 76.7 us
  blocking collectives: 22.6 us -> 84.9 us
  local copies, waits for them, and re-layouts: 8.63 us -> 53.1 us
    reduce_scatter x4 -> x2, waiting for transfers between devices: 948 us -> 0.02 us  [weight_grad(): lax.psum_scatter(own, 'chip', scatter_dimension=0, tiled=True).astype(BF)]
    all_gather x4 -> x6, waiting for transfers between devices: 455 us -> 275 us  [gather(): return lax.all_gather(rows, axes, axis=0, tiled=True)]
    dot_general x23 -> x16, matrix products: 463 us -> 362 us  [the longest x5 148 us: dot_nn(): lax.dot_general(a, b, (((1,), (0,)), ((), ())), preferred_element_type=F32)]
    ppermute x0 -> x16, waiting for transfers between devices: none -> 80.9 us  [the longest x14 72.9 us: to_tokens(): got = lax.ppermute(piece(me ^ k), TP, [(i, i ^ k) for i in range(tp)])]
    pallas_call x0 -> x2, Pallas kernels: none -> 76.7 us  [attention_call(): pl.pallas_call(body, grid=(images, steps), in_specs=[spec(a.shape[1]) for...]
    all_gather x0 -> x1, blocking collectives: none -> 61.3 us  [layer_step(): b_rows = lax.all_gather(b_own, ('core', 'chip'), axis=0, tiled=False)]
    transpose x0 -> x2, local copies, waits for them, and re-layouts: none -> 25.1 us  [the longest x1 23.1 us: layer_step(): d_ord = d_stack.transpose(1, 0, 2, 3).reshape(images * tp * toks, width)]
  transfers between devices with their start and end apart: 8 -> 25, of which waited for: 8 -> 10; matrix products, arithmetic and copies ran while one was open for 9% -> 35% of each run, Pallas kernels for 0% -> 8%
where the time goes in v1:
time: 1020 us; the launch traced here: 1010 us
  matrix products  362 us (35%)
  waiting for transfers between devices  359 us (35%)
  blocking collectives  84.9 us (8%)
  Pallas kernels  76.7 us (8%)
  local copies, waits for them, and re-layouts  53.1 us (5%)
  other arithmetic  39.6 us (4%)
  starting transfers between devices  18.5 us (2%)
  between operations  15.3 us (2%)
    all_gather x6, waiting for transfers between devices, gather(): return lax.all_gather(rows, axes, axis=0, tiled=True)  275 us
    dot_general x5, matrix products, dot_nn(): lax.dot_general(a, b, (((1,), (0,)), ((), ())), preferred_element_type=F32)  148 us
    dot_general x5, matrix products, dot_nt(): lax.dot_general(a, b, (((1,), (1,)), ((), ())), preferred_element_type=F32)  107 us
    dot_general x6, matrix products, dot_tn(): lax.dot_general(a, b, (((0,), (0,)), ((), ())), preferred_element_type=F32)  107 us
    pallas_call x2, Pallas kernels, attention_call(): pl.pallas_call(body, grid=(images, steps), in_specs=[spec(a.shape[1]) for...  76.7 us
    ppermute x14, waiting for transfers between devices, to_tokens(): got = lax.ppermute(piece(me ^ k), TP, [(i, i ^ k) for i in range(tp)])  72.9 us
    all_gather x1, blocking collectives, layer_step(): b_rows = lax.all_gather(b_own, ('core', 'chip'), axis=0, tiled=False)  61.3 us
    psum x1, blocking collectives, layer_step(): vec_sums = lax.psum(vec_parts.reshape(9, width), TP).reshape(9 * width)  23.6 us
  transfers between devices with their start and end apart: 25, of which 10 were waited for; matrix products, arithmetic and copies ran while one was open for 35% of the time, Pallas kernels for 8%

profile of v1, /device:TPU:0, one launch (start us, length us, event | category | flops | bytes accessed | tf_op | source)
XLA Modules:
  0.0 1008.3 jit_solution(13473814021019148606)
XLA Ops:
  7.2 2.7 pad_maximum_fusion
  12.7 4.3 all-to-all-start
  17.3 61.3 %all-gather.1 = f32[8,14,96]{2,1,0:T(8,128)S(1)} all-gather(f32[1,14,96]{2,1,0:T(8,128)S(1)} %maximum_bitcast_fusion), channel_id=2, replica_groups=mesh['dp'=1,'chip'=4,'core'=2] {'core','chip'}, dimensions={0}, use_global_device_ids=true | all-gather | bytes 48384 | tf_op jit(solution)/shard_map/all_gather | solution.py:170
  78.8 3.5 copy.40
  83.2 2.6 copy-done
  86.3 3.5 fusion.49
  91.1 3.5 add_convert_fusion.4
  94.6 23.6 %all-gather.9.cloned.1.call-done = bf16[4608,1536]{1,0:T(8,128)(2,1)} async-done(((bf16[576,1536]{1,0:T(8,128)(2,1)}), bf16[4608,1536]{1,0:T(8,128)(2,1)}) %all-gather.9.cloned.1.call-update) | async-done | bytes 14155792 | tf_op jit(solution)/shard_map/all_gather | solution.py:121
  118.2 19.4 %add_convert_fusion.2.qkv_ref = bf16[1024,4608]{1,0:T(8,128)(2,1)} fusion(bf16[1024,1536]{1,0:T(8,128)(2,1)S(1)} %add_convert_fusion.4, bf16[4608,1536]{1,0:T(8,128)(2,1)} %all-gather.9.cloned.1.call-done, f32[4608]{0:T(1024)S(1)} %add.213), kind=kOutput, calls=%fused_computation.37 | convolution fusion | flops 14504951808 | bytes 26757120 | tf_op jit(solution)/shard_map/dot_general | solution.py:87
  137.6 29.8 %shard_map.296 = bf16[1024,1536]{1,0:T(8,128)(2,1)} custom-call(bf16[1024,4608]{1,0:T(8,128)(2,1)} %add_convert_fusion.2.qkv_ref), custom_call_target="tpu_custom_call" | custom-call | flops 1610612736 | bytes 12582912 | tf_op jit(solution)/shard_map/pallas_call | solution.py:76
  167.3 9.2 convert_reduce_fusion.3
  178.7 2.7 fusion.37
  181.4 66.4 %all-gather.13.cloned.1.call-done = bf16[6144,1536]{0,1:T(8,128)(2,1)} async-done(((bf16[768,1536]{0,1:T(8,128)(2,1)}), bf16[6144,1536]{0,1:T(8,128)(2,1)}) %all-gather.13.cloned.1.call-update) | async-done | bytes 18874384 | tf_op jit(solution)/shard_map/all_gather | solution.py:121
  247.8 26.0 %add_convert_fusion.1 = bf16[1024,6144]{1,0:T(8,128)(2,1)} fusion(bf16[1024,1536]{1,0:T(8,128)(2,1)} %fusion.37, bf16[6144,1536]{0,1:T(8,128)(2,1)} %all-gather.13.cloned.1.call-done, f32[6144]{0:T(1024)S(1)} %add.222), kind=kOutput, calls=%fused_computation.35 | convolution fusion | flops 19339935744 | bytes 34627584 | tf_op jit(solution)/shard_map/dot_general | solution.py:87
  273.7 95.4 %all-gather.17.cloned.1.call-done = bf16[256,32,1536]{2,1,0:T(8,128)(2,1)} async-done(((bf16[32,32,1536]{2,1,0:T(8,128)(2,1)}), bf16[256,32,1536]{2,1,0:T(8,128)(2,1)}) %all-gather.17.cloned.1.call-update) | async-done | bytes 25165840 | tf_op jit(solution)/shard_map/all_gather | solution.py:121
  369.1 3.4 convert_reduce_fusion.5
  372.5 2.0 copy.41
  374.5 89.3 %all-gather.15.cloned.1.call-done = bf16[6144,1536]{1,0:T(8,128)(2,1)} async-done(((bf16[768,1536]{1,0:T(8,128)(2,1)}), bf16[6144,1536]{1,0:T(8,128)(2,1)}) %all-gather.15.cloned.1.call-update) | async-done | bytes 18874384 | tf_op jit(solution)/shard_map/all_gather | solution.py:121
  463.8 25.9 %convolution_convert_fusion.1 = bf16[1024,6144]{1,0:T(8,128)(2,1)} fusion(bf16[1024,1536]{1,0:T(8,128)(2,1)} %bitcast.100, bf16[6144,1536]{1,0:T(8,128)(2,1)} %all-gather.15.cloned.1.call-done), kind=kOutput, calls=%fused_computation.43 | convolution fusion | flops 19333644288 | bytes 34603008 | tf_op jit(solution)/shard_map/dot_general | solution.py:87
  489.7 39.7 %convert_reduce_fusion.2 = (f32[1536]{0:T(1024)}, f32[1024]{0:T(1024)S(1)}, bf16[1024,1536]{1,0:T(8,128)(2,1)S(1)}) fusion(f32[1536]{0:T(1024)S(1)} %copy-done.9, f32[1024]{0:T(1024)S(1)} %broadcast_multiply_fusion.1, bf16[1024,1536]{1,0:T(8,128)(2,1)S(1)} %get-tuple-element.65, bf16[6144,1536]{0,1:T(8,128)(2,1)} %all-gather.13.cloned.1.call-done, ...), kind=kOutput, calls=%fused_computation.49 | convolution fusion | flops 19478343680 | bytes 50352128 | tf_op jit(solution)/shard_map/dot_general | solution.py:91
  529.5 4.1 fusion.44
  533.6 3.6 convert_reduce_fusion.4
  538.8 4.2 fusion.62
  543.3 8.0 collective-permute-done.15
  551.3 8.6 convolution_add_fusion.1
  560.8 9.4 convolution_convert_fusion.3.da_ref
  570.2 46.9 %shard_map.297 = bf16[1024,4608]{1,0:T(8,128)(2,1)} custom-call(bf16[1024,4608]{1,0:T(8,128)(2,1)} %add_convert_fusion.2.qkv_ref, bf16[1024,1536]{1,0:T(8,128)(2,1)} %convolution_convert_fusion.3.da_ref), custom_call_target="tpu_custom_call" | custom-call | flops 4026531840 | bytes 22020096 | tf_op jit(solution)/shard_map/pallas_call | solution.py:76
  617.1 14.9 %fusion.52 = f32[2304,1536]{1,0:T(8,128)} fusion(bf16[1024,1536]{1,0:T(8,128)(2,1)} %copy-done.7, bf16[1024,4608]{1,0:T(8,128)(2,1)} %shard_map.297, s32[]{:T(128)S(6)} %select_n.97), kind=kOutput, calls=%fused_computation.86 | convolution fusion | flops 7247757312 | bytes 22020100 | tf_op jit(solution)/shard_map/dot_general | solution.py:95
  632.3 30.0 %fusion.43 = bf16[1024,1536]{1,0:T(8,128)(2,1)S(1)} fusion(bf16[1024,1536]{1,0:T(8,128)(2,1)S(1)} %get-tuple-element.65, bf16[6144,1536]{1,0:T(8,128)(2,1)} %all-gather.15.cloned.1.call-done, bf16[1024,6144]{1,0:T(8,128)(2,1)} %add_convert_fusion.1, f32[1536]{0:T(1024)S(1)} %convert_element_type.165), kind=kOutput, calls=%fused_computation.72 | convolution fusion | flops 19396558848 | bytes 37754880 | tf_op jit(solution)/shard_map/dot_general | solution.py:91
  669.1 16.2 %collective-permute-done.1 = bf16[4,32,1536]{2,1,0:T(8,128)(2,1)} collective-permute-done((bf16[4,32,1536]{2,1,0:T(8,128)(2,1)}, bf16[4,32,1536]{2,1,0:T(8,128)(2,1)}, u32[]{:S(2)}, u32[]{:S(2)}) %collective-permute-start.1) | collective-permute-done | bytes 393248 | tf_op jit(solution)/shard_map/ppermute | solution.py:148
  687.8 13.5 %collective-permute-done.2 = bf16[4,32,1536]{2,1,0:T(8,128)(2,1)S(1)} collective-permute-done((bf16[4,32,1536]{2,1,0:T(8,128)(2,1)}, bf16[4,32,1536]{2,1,0:T(8,128)(2,1)S(1)}, u32[]{:S(2)}, u32[]{:S(2)}) %collective-permute-start.2) | collective-permute-done | bytes 393248 | tf_op jit(solution)/shard_map/ppermute | solution.py:148
  701.2 2.1 collective-permute-start.6
  703.4 16.8 %convolution_add_fusion = f32[2304,1536]{1,0:T(8,128)} fusion(f32[2304,1536]{1,0:T(8,128)} %collective-permute-done.14, bf16[1024,1536]{1,0:T(8,128)(2,1)} %copy-done.7, bf16[1024,4608]{1,0:T(8,128)(2,1)} %shard_map.297, s32[]{:T(128)S(6)} %select_n.96), kind=kOutput, calls=%fused_computation.39 | convolution fusion | flops 7251296256 | bytes 36175876 | tf_op jit(solution)/shard_map/dot_general | solution.py:95
  725.7 9.6 collective-permute-done.6
  737.1 21.8 %convert_reduce_fusion.1 = (f32[1536]{0:T(1024)S(1)}, f32[1024]{0:T(1024)S(1)}, bf16[1024,1536]{1,0:T(8,128)(2,1)S(1)}) fusion(f32[1536]{0:T(1024)S(1)} %copy-done.11, f32[1024]{0:T(1024)S(1)} %copy-done.15, f32[8,4,32,1536]{3,2,0,1:T(8,128)} %copy.40, bf16[1024,4608]{1,0:T(8,128)(2,1)} %shard_map.297, bf16[4608,1536]{1,0:T(8,128)(2,1)} %all-gather.9.cloned.1.call-done), kind=kOutput, calls=%fused_computation.45 | convolution fusion | flops 14506521600 | bytes 33050624 | tf_op jit(solution)/shard_map/dot_general | solution.py:91
  758.9 4.1 fusion.45
  763.1 3.1 fusion.39
  770.6 23.1 %copy.42 = bf16[32,8,32,1536]{3,2,1,0:T(8,128)(2,1)} copy(bf16[32,8,32,1536]{3,2,0,1:T(8,128)(2,1)} %bitcast.95) | data formatting | bytes 50331648 | tf_op jit(solution)/shard_map/transpose | solution.py:220
  795.4 26.1 %convolution_convert_fusion = bf16[8192,768]{1,0:T(8,128)(2,1)} fusion(bf16[8192,1536]{1,0:T(8,128)(2,1)} %bitcast.97, bf16[768,1536]{1,0:T(8,128)(2,1)S(1)} %copy-done.8), kind=kOutput, calls=%fused_computation.38 | convolution fusion | flops 19333644288 | bytes 40108032 | tf_op jit(solution)/shard_map/dot_general | solution.py:87
  821.6 2.2 collective-permute-start.12
  825.3 17.6 %collective-permute-done.12 = bf16[4,32,1536]{2,1,0:T(8,128)(2,1)S(1)} collective-permute-done((bf16[4,32,1536]{2,1,0:T(8,128)(2,1)S(1)}, bf16[4,32,1536]{2,1,0:T(8,128)(2,1)S(1)}, u32[]{:S(2)}, u32[]{:S(2)}) %collective-permute-start.12) | collective-permute-done | bytes 393248 | tf_op jit(solution)/shard_map/ppermute | solution.py:148
  843.0 15.9 %collective-permute-done.13 = bf16[4,32,1536]{2,1,0:T(8,128)(2,1)S(1)} collective-permute-done((bf16[4,32,1536]{2,1,0:T(8,128)(2,1)S(1)}, bf16[4,32,1536]{2,1,0:T(8,128)(2,1)S(1)}, u32[]{:S(2)}, u32[]{:S(2)}) %collective-permute-start.13) | collective-permute-done | bytes 393248 | tf_op jit(solution)/shard_map/ppermute | solution.py:148
  859.0 3.0 convert_element_type.191
  862.0 47.3 %fusion.85 = (bf16[768]{0:T(1024)(128)(2,1)}, bf16[8192,768]{1,0:T(8,128)(2,1)}, bf16[8192,768]{1,0:T(8,128)(2,1)}) fusion(bf16[8192,768]{1,0:T(8,128)(2,1)} %convolution_convert_fusion, f32[768]{0:T(1024)S(1)} %convert_element_type.156, bf16[8192,1536]{1,0:T(8,128)(2,1)} %all-gather.19.cloned.1.call-done, bf16[1536,768]{1,0:T(8,128)(2,1)} %param.30), kind=kOutput, calls=%fused_computation.174 | convolution fusion | flops 19484639232 | bytes 65278464 | tf_op jit(solution)/shard_map/dot_general | solution.py:91
  909.3 26.2 %convolution_convert_fusion.4 = bf16[1536,768]{1,0:T(8,128)(2,1)} fusion(bf16[8192,1536]{1,0:T(8,128)(2,1)} %all-gather.19.cloned.1.call-done, bf16[8192,768]{1,0:T(8,128)(2,1)} %get-tuple-element.38), kind=kOutput, calls=%fused_computation.95 | convolution fusion | flops 19328532480 | bytes 40108032 | tf_op jit(solution)/shard_map/dot_general | solution.py:95
  935.4 36.0 %fusion.59 = bf16[768,1536]{1,0:T(8,128)(2,1)} fusion(bf16[8192,1536]{1,0:T(8,128)(2,1)} %bitcast.98, bf16[8192,768]{1,0:T(8,128)(2,1)} %get-tuple-element.68), kind=kOutput, calls=%fused_computation.94 | convolution fusion | flops 19391447040 | bytes 40108032 | tf_op jit(solution)/shard_map/dot_general | solution.py:95
  971.4 23.6 %psum.7 = f32[9,1536]{1,0:T(8,128)S(1)} all-reduce(f32[9,1536]{1,0:T(8,128)S(1)} %reshape.213), channel_id=1, replica_groups=mesh['dp'=1,'chip'=4,'core'=2] {'chip','core'}, use_global_device_ids=true, to_apply=%region_15.0 | all-reduce | flops 13824 | bytes 110592 | tf_op jit(solution)/shard_map/psum | solution.py:229
  997.7 2.2 convert_element_type.189
  (195 shorter events, 38.7 us)
Async XLA Ops:
  7.2 111.0 %all-gather.9.cloned.1.call-start = ((), (), s32[]{:S(2)}) async-start(), calls=%async_computation.3 | async-start | bytes 15925248 | tf_op jit(solution)/shard_map/all_gather | solution.py:121
  10.0 157.3 %all-gather.11.cloned.1.call-start = ((), (), s32[]{:S(2)}) async-start(), calls=%async_computation.4 | async-start | bytes 5308416 | tf_op jit(solution)/shard_map/all_gather | solution.py:121
  10.8 237.0 %all-gather.13.cloned.1.call-start = ((), (), s32[]{:S(2)}) async-start(), calls=%async_computation.5 | async-start | bytes 21233664 | tf_op jit(solution)/shard_map/all_gather | solution.py:121
  11.5 67.1 %copy-start.33 = (bf16[1536]{0:T(1024)(128)(2,1)S(1)}, bf16[1536]{0:T(1024)(128)(2,1)}, u32[]{:S(2)}) copy-start(bf16[1536]{0:T(1024)(128)(2,1)} %param.27) | copy-start | bytes 9220
  11.5 357.6 %all-gather.17.cloned.1.call-start = ((), (), s32[]{:S(2)}) async-start(), calls=%async_computation.7 | async-start | bytes 28311552 | tf_op jit(solution)/shard_map/all_gather | solution.py:121
  12.1 451.7 %all-gather.15.cloned.1.call-start = ((), (), s32[]{:S(2)}) async-start(), calls=%async_computation.6 | async-start | bytes 21233664 | tf_op jit(solution)/shard_map/all_gather | solution.py:121
  12.7 66.1 %all-to-all-start = ((bf16[32,32,1536]{2,1,0:T(8,128)(2,1)}), bf16[32,32,1536]{2,1,0:T(8,128)(2,1)S(1)}, u32[]{:S(2)}, u32[]{:S(2)}) async-start(bf16[32,32,1536]{2,1,0:T(8,128)(2,1)} %param.17), calls=%async_computation | async-start | bytes 6291456 | tf_op jit(solution)/shard_map/all_to_all | solution.py:135
  17.0 842.0 %reduce-scatter.5.cloned.1.call-start = ((), (), s32[]{:S(2)}) async-start(), calls=%async_computation.10 | async-start | bytes 5898240 | tf_op jit(solution)/shard_map/reduce_scatter | solution.py:132
  94.6 43.0 %copy-start.7 = (bf16[1024,1536]{1,0:T(8,128)(2,1)}, bf16[1024,1536]{1,0:T(8,128)(2,1)S(1)}, u32[]{:S(2)}) copy-start(bf16[1024,1536]{1,0:T(8,128)(2,1)S(1)} %add_convert_fusion.4) | copy-start | bytes 9437188
  489.7 39.7 %copy-start.22 = (f32[1024]{0:T(1024)S(1)}, f32[1024]{0:T(1024)}, u32[]{:S(2)}) copy-start(f32[1024]{0:T(1024)} %copy-done.21) | copy-start | bytes 12292
  489.7 39.8 %copy-start.13 = (f32[1024]{0:T(1024)S(1)}, f32[1024]{0:T(1024)}, u32[]{:S(2)}) copy-start(f32[1024]{0:T(1024)} %copy-done.12) | copy-start | bytes 12292
  543.1 8.3 collective-permute-start.15
  560.0 302.0 %all-gather.19.cloned.1.call-start = ((), (), s32[]{:S(2)}) async-start(), calls=%async_computation.8 | async-start | bytes 28311552 | tf_op jit(solution)/shard_map/all_gather | solution.py:121
  560.7 436.9 %reduce-scatter.3.cloned.1.call-start = ((), (), s32[]{:S(2)}) async-start(), calls=%async_computation.9 | async-start | bytes 17694720 | tf_op jit(solution)/shard_map/reduce_scatter | solution.py:132
  617.1 15.1 %copy-start.34 = (bf16[1536]{0:T(1024)(128)(2,1)S(1)}, bf16[1536]{0:T(1024)(128)(2,1)}, u32[]{:S(2)}) copy-start(bf16[1536]{0:T(1024)(128)(2,1)} %param.33) | copy-start | bytes 9220
  632.1 71.3 %collective-permute-start.14 = (f32[2304,1536]{1,0:T(8,128)}, f32[2304,1536]{1,0:T(8,128)}, u32[]{:S(2)}, u32[]{:S(2)}) collective-permute-start(f32[2304,1536]{1,0:T(8,128)} %fusion.52), channel_id=1, source_target_pairs={{0,1},{1,0},{2,3},{3,2},{4,5},{5,4},{6,7},{7,6}} | collective-permute-start | bytes 42467336 | tf_op jit(solution)/shard_map/ppermute | solution.py:130
  664.2 2.7 collective-permute-start
  664.6 20.7 %collective-permute-start.1 = (bf16[4,32,1536]{2,1,0:T(8,128)(2,1)}, bf16[4,32,1536]{2,1,0:T(8,128)(2,1)}, u32[]{:S(2)}, u32[]{:S(2)}) collective-permute-start(bf16[4,32,1536]{2,1,0:T(8,128)(2,1)} %get-tuple-element.56), channel_id=1, source_target_pairs={{0,2},{1,3},{2,0},{3,1},{4,6},{5,7},{6,4},{7,5}} | collective-permute-start | bytes 1179656 | tf_op jit(solution)/shard_map/ppermute | solution.py:148
  666.1 35.1 %collective-permute-start.2 = (bf16[4,32,1536]{2,1,0:T(8,128)(2,1)}, bf16[4,32,1536]{2,1,0:T(8,128)(2,1)S(1)}, u32[]{:S(2)}, u32[]{:S(2)}) collective-permute-start(bf16[4,32,1536]{2,1,0:T(8,128)(2,1)} %get-tuple-element.55), channel_id=1, source_target_pairs={{0,3},{1,2},{2,1},{3,0},{4,7},{5,6},{6,5},{7,4}} | collective-permute-start | bytes 1179656 | tf_op jit(solution)/shard_map/ppermute | solution.py:148
  666.1 54.1 %collective-permute-start.3 = (bf16[4,32,1536]{2,1,0:T(8,128)(2,1)}, bf16[4,32,1536]{2,1,0:T(8,128)(2,1)}, u32[]{:S(2)}, u32[]{:S(2)}) collective-permute-start(bf16[4,32,1536]{2,1,0:T(8,128)(2,1)} %get-tuple-element.54), channel_id=1, source_target_pairs={{0,4},{1,5},{2,6},{3,7},{4,0},{5,1},{6,2},{7,3}} | collective-permute-start | bytes 1179656 | tf_op jit(solution)/shard_map/ppermute | solution.py:148
  666.9 55.2 %collective-permute-start.4 = (bf16[4,32,1536]{2,1,0:T(8,128)(2,1)}, bf16[4,32,1536]{2,1,0:T(8,128)(2,1)}, u32[]{:S(2)}, u32[]{:S(2)}) collective-permute-start(bf16[4,32,1536]{2,1,0:T(8,128)(2,1)} %get-tuple-element.53), channel_id=1, source_target_pairs={{0,5},{1,4},{2,7},{3,6},{4,1},{5,0},{6,3},{7,2}} | collective-permute-start | bytes 1179656 | tf_op jit(solution)/shard_map/ppermute | solution.py:148
  685.3 38.6 %collective-permute-start.5 = (bf16[4,32,1536]{2,1,0:T(8,128)(2,1)}, bf16[4,32,1536]{2,1,0:T(8,128)(2,1)}, u32[]{:S(2)}, u32[]{:S(2)}) collective-permute-start(bf16[4,32,1536]{2,1,0:T(8,128)(2,1)} %get-tuple-element.52), channel_id=1, source_target_pairs={{0,6},{1,7},{2,4},{3,5},{4,2},{5,3},{6,0},{7,1}} | collective-permute-start | bytes 1179656 | tf_op jit(solution)/shard_map/ppermute | solution.py:148
  701.2 34.0 %collective-permute-start.6 = (bf16[4,32,1536]{2,1,0:T(8,128)(2,1)S(1)}, bf16[4,32,1536]{2,1,0:T(8,128)(2,1)}, u32[]{:S(2)}, u32[]{:S(2)}) collective-permute-start(bf16[4,32,1536]{2,1,0:T(8,128)(2,1)S(1)} %get-tuple-element.51), channel_id=1, source_target_pairs={{0,7},{1,6},{2,5},{3,4},{4,3},{5,2},{6,1},{7,0}} | collective-permute-start | bytes 1179656 | tf_op jit(solution)/shard_map/ppermute | solution.py:148
  703.3 16.8 %copy-start.6 = (bf16[32,32,1536]{2,1,0:T(8,128)(2,1)}, bf16[32,32,1536]{2,1,0:T(8,128)(2,1)S(1)}, u32[]{:S(2)}) copy-start(bf16[32,32,1536]{2,1,0:T(8,128)(2,1)S(1)} %constant_dynamic-update-slice_fusion.11) | copy-start | bytes 9437188
  720.2 16.9 %copy-start.11 = (f32[1536]{0:T(1024)S(1)}, f32[1536]{0:T(1024)}, u32[]{:S(2)}) copy-start(f32[1536]{0:T(1024)} %param.19) | copy-start | bytes 18436
  720.2 16.9 %copy-start.15 = (f32[1024]{0:T(1024)S(1)}, f32[1024]{0:T(1024)}, u32[]{:S(2)}) copy-start(f32[1024]{0:T(1024)} %copy-done.14) | copy-start | bytes 12292
  720.2 38.7 %slice-start = ((s8[6291456]{0:T(1024)(128)(4,1)}), s8[2097152]{0:T(1024)(128)(4,1)S(1)}, s32[]{:S(2)}) async-start(s8[6291456]{0:T(1024)(128)(4,1)} %bitcast.90), calls=%async_computation.11 | async-start | bytes 4194304
  737.0 21.8 %copy-start.24 = (f32[1024]{0:T(1024)S(1)}, f32[1024]{0:T(1024)}, u32[]{:S(2)}) copy-start(f32[1024]{0:T(1024)} %copy-done.23) | copy-start | bytes 12292
  737.0 21.9 %slice-start.1 = ((s8[6291456]{0:T(1024)(128)(4,1)}), s8[4194304]{0:T(1024)(128)(4,1)S(1)}, s32[]{:S(2)}) async-start(s8[6291456]{0:T(1024)(128)(4,1)} %bitcast.90), calls=%async_computation.12 | async-start | bytes 8388608
  737.1 21.9 %copy-start.17 = (f32[1024]{0:T(1024)S(1)}, f32[1024]{0:T(1024)}, u32[]{:S(2)}) copy-start(f32[1024]{0:T(1024)} %copy-done.16) | copy-start | bytes 12292
  766.8 54.8 %collective-permute-start.7 = (bf16[4,32,1536]{2,1,0:T(8,128)(2,1)S(1)}, bf16[4,32,1536]{2,1,0:T(8,128)(2,1)}, u32[]{:S(2)}, u32[]{:S(2)}) collective-permute-start(bf16[4,32,1536]{2,1,0:T(8,128)(2,1)S(1)} %get-tuple-element.49), channel_id=1, source_target_pairs={{0,1},{1,0},{2,3},{3,2},{4,5},{5,4},{6,7},{7,6}} | collective-permute-start | bytes 1179656 | tf_op jit(solution)/shard_map/ppermute | solution.py:148
  767.0 57.8 %collective-permute-start.8 = (bf16[4,32,1536]{2,1,0:T(8,128)(2,1)S(1)}, bf16[4,32,1536]{2,1,0:T(8,128)(2,1)S(1)}, u32[]{:S(2)}, u32[]{:S(2)}) collective-permute-start(bf16[4,32,1536]{2,1,0:T(8,128)(2,1)S(1)} %get-tuple-element.48), channel_id=1, source_target_pairs={{0,2},{1,3},{2,0},{3,1},{4,6},{5,7},{6,4},{7,5}} | collective-permute-start | bytes 1179656 | tf_op jit(solution)/shard_map/ppermute | solution.py:148
  768.4 56.7 %collective-permute-start.9 = (bf16[4,32,1536]{2,1,0:T(8,128)(2,1)S(1)}, bf16[4,32,1536]{2,1,0:T(8,128)(2,1)S(1)}, u32[]{:S(2)}, u32[]{:S(2)}) collective-permute-start(bf16[4,32,1536]{2,1,0:T(8,128)(2,1)S(1)} %get-tuple-element.47), channel_id=1, source_target_pairs={{0,3},{1,2},{2,1},{3,0},{4,7},{5,6},{6,5},{7,4}} | collective-permute-start | bytes 1179656 | tf_op jit(solution)/shard_map/ppermute | solution.py:148
  768.7 56.5 %collective-permute-start.10 = (bf16[4,32,1536]{2,1,0:T(8,128)(2,1)S(1)}, bf16[4,32,1536]{2,1,0:T(8,128)(2,1)S(1)}, u32[]{:S(2)}, u32[]{:S(2)}) collective-permute-start(bf16[4,32,1536]{2,1,0:T(8,128)(2,1)S(1)} %get-tuple-element.46), channel_id=1, source_target_pairs={{0,4},{1,5},{2,6},{3,7},{4,0},{5,1},{6,2},{7,3}} | collective-permute-start | bytes 1179656 | tf_op jit(solution)/shard_map/ppermute | solution.py:148
  770.0 55.2 %collective-permute-start.11 = (bf16[4,32,1536]{2,1,0:T(8,128)(2,1)S(1)}, bf16[4,32,1536]{2,1,0:T(8,128)(2,1)S(1)}, u32[]{:S(2)}, u32[]{:S(2)}) collective-permute-start(bf16[4,32,1536]{2,1,0:T(8,128)(2,1)S(1)} %get-tuple-element.45), channel_id=1, source_target_pairs={{0,5},{1,4},{2,7},{3,6},{4,1},{5,0},{6,3},{7,2}} | collective-permute-start | bytes 1179656 | tf_op jit(solution)/shard_map/ppermute | solution.py:148
  770.5 23.2 %slice-start.2 = ((s8[9437184]{0:T(1024)(128)(4,1)}), s8[4194304]{0:T(1024)(128)(4,1)S(1)}, s32[]{:S(2)}) async-start(s8[9437184]{0:T(1024)(128)(4,1)} %bitcast.92), calls=%async_computation.13 | async-start | bytes 8388608
  770.5 23.2 %copy-start.18 = (f32[13824]{0:T(1024)S(1)}, f32[13824]{0:T(1024)}, u32[]{:S(2)}) copy-start(f32[13824]{0:T(1024)} %custom-call) | copy-start | bytes 165892
  770.5 23.2 %copy-start.27 = (f32[1536]{0:T(1024)S(1)}, f32[1536]{0:T(1024)}, u32[]{:S(2)}) copy-start(f32[1536]{0:T(1024)} %get-tuple-element.41) | copy-start | bytes 18436
  770.5 23.2 %slice-start.3 = ((s8[9437184]{0:T(1024)(128)(4,1)}), s8[4194304]{0:T(1024)(128)(4,1)S(1)}, s32[]{:S(2)}) async-start(s8[9437184]{0:T(1024)(128)(4,1)} %bitcast.92), calls=%async_computation.14 | async-start | bytes 8388608
  770.5 23.2 %slice-start.4 = ((s8[9437184]{0:T(1024)(128)(4,1)}), s8[1048576]{0:T(1024)(128)(4,1)S(1)}, s32[]{:S(2)}) async-start(s8[9437184]{0:T(1024)(128)(4,1)} %bitcast.92), calls=%async_computation.15 | async-start | bytes 2097152
  795.4 26.1 %copy-start.26 = (f32[1536]{0:T(1024)S(1)}, f32[1536]{0:T(1024)}, u32[]{:S(2)}) copy-start(f32[1536]{0:T(1024)} %get-tuple-element.25) | copy-start | bytes 18436
  795.4 26.1 %copy-start.31 = (f32[1536]{0:T(1024)S(1)}, f32[1536]{0:T(1024)}, u32[]{:S(2)}) copy-start(f32[1536]{0:T(1024)} %get-tuple-element.27) | copy-start | bytes 18436
  795.4 26.2 %copy-start.25 = (f32[1536]{0:T(1024)S(1)}, f32[1536]{0:T(1024)}, u32[]{:S(2)}) copy-start(f32[1536]{0:T(1024)} %get-tuple-element.39) | copy-start | bytes 18436
  821.6 37.3 %copy-start.19 = (f32[13824]{0:T(1024)}, f32[13824]{0:T(1024)S(1)}, u32[]{:S(2)}) copy-start(f32[13824]{0:T(1024)S(1)} %constant_dynamic-update-slice_fusion.14) | copy-start | bytes 165892
  821.6 21.3 %collective-permute-start.12 = (bf16[4,32,1536]{2,1,0:T(8,128)(2,1)S(1)}, bf16[4,32,1536]{2,1,0:T(8,128)(2,1)S(1)}, u32[]{:S(2)}, u32[]{:S(2)}) collective-permute-start(bf16[4,32,1536]{2,1,0:T(8,128)(2,1)S(1)} %get-tuple-element.44), channel_id=1, source_target_pairs={{0,6},{1,7},{2,4},{3,5},{4,2},{5,3},{6,0},{7,1}} | collective-permute-start | bytes 1179656 | tf_op jit(solution)/shard_map/ppermute | solution.py:148
  824.8 34.1 %collective-permute-start.13 = (bf16[4,32,1536]{2,1,0:T(8,128)(2,1)S(1)}, bf16[4,32,1536]{2,1,0:T(8,128)(2,1)S(1)}, u32[]{:S(2)}, u32[]{:S(2)}) collective-permute-start(bf16[4,32,1536]{2,1,0:T(8,128)(2,1)S(1)} %get-tuple-element.43), channel_id=1, source_target_pairs={{0,7},{1,6},{2,5},{3,4},{4,3},{5,2},{6,1},{7,0}} | collective-permute-start | bytes 1179656 | tf_op jit(solution)/shard_map/ppermute | solution.py:148
  858.9 50.3 %copy-start.5 = (bf16[32,32,1536]{2,1,0:T(8,128)(2,1)}, bf16[32,32,1536]{2,1,0:T(8,128)(2,1)S(1)}, u32[]{:S(2)}) copy-start(bf16[32,32,1536]{2,1,0:T(8,128)(2,1)S(1)} %constant_dynamic-update-slice_fusion) | copy-start | bytes 9437188
  935.4 36.0 %copy-start.20 = (f32[13824]{0:T(1024)S(1)}, f32[13824]{0:T(1024)}, u32[]{:S(2)}) copy-start(f32[13824]{0:T(1024)} %copy-done.19) | copy-start | bytes 165892
  (19 other events, 84.2 us)
Sparse Core Ops, SparseCore 0:
  10.4 107.7 all-gather.8
  120.0 33.2 all-gather.10
  155.1 92.6 all-gather.12
  249.4 119.6 all-gather.16
  370.8 93.0 all-gather.14
  560.1 51.4 reduce-scatter.4
  613.4 153.3 all-gather.18
  769.8 158.6 reduce-scatter.2
